TPU v7x, 32 devices: a 4x4x1 block of a 4x4x8 slice. The times are simulated.
32 devices in a mesh: dp: 1 (over z), tp: 4 (over y), ctx: 8 (over x, core).
Axes of the slice: x: 4, y: 4, z: 1, core: 2. Of those that a mesh axis runs over, the one named last changes fastest.
The devices are a block of a 4x4x8 slice.
Arguments:
- hidden: bfloat16 [1024, 8192], P(('dp', 'ctx'))
- w_q: bfloat16 [8192, 8192], P(None, 'tp')
- w_k: bfloat16 [8192, 1024], P(None, 'tp')
- w_v: bfloat16 [8192, 1024], P(None, 'tp')
- w_o: bfloat16 [8192, 8192], P('tp')
- k_prefix: bfloat16 [2048, 8, 128], P(('dp', 'ctx'), 'tp')
- v_prefix: bfloat16 [2048, 8, 128], P(('dp', 'ctx'), 'tp')
- k_suffix: bfloat16 [1024, 256, 8, 128], P(('dp', 'ctx'), None, 'tp')
- v_suffix: bfloat16 [1024, 256, 8, 128], P(('dp', 'ctx'), None, 'tp')
- seq_lens: int32 [1024], P(('dp', 'ctx'))
Outputs:
- output: bfloat16 [1024, 8192], P(('dp', 'ctx'))
All inputs are finite; a program needn't handle non-finite values.
Results may differ from a plain program's by a relative error of at most 0.00452208.
Values are sent between devices in bfloat16 or wider.
A program may use at most 768 MiB of HBM per device.

v0:
```python
import jax
import jax.numpy as jnp
from jax import lax
from jax.sharding import PartitionSpec as P, NamedSharding


def solution(mesh):
    ctx_size = mesh.shape['ctx']
    row_axes = ('dp', 'ctx')

    def device_step(hidden, w_q, w_k, w_v, w_o, k_prefix, v_prefix, k_suffix, v_suffix, seq_lens):
        seq_count = hidden.shape[0]
        kv_local = k_prefix.shape[1]
        head_dim = k_prefix.shape[2]
        group_size = w_q.shape[1] // (kv_local * head_dim)
        score_scale = head_dim ** -0.5
        q_local = jnp.dot(hidden, w_q, preferred_element_type=jnp.float32).astype(jnp.bfloat16)
        q_local = q_local.reshape(seq_count, kv_local, group_size, head_dim)
        k_new = jnp.dot(hidden, w_k, preferred_element_type=jnp.float32).astype(jnp.bfloat16).reshape(seq_count, kv_local, head_dim)
        v_new = jnp.dot(hidden, w_v, preferred_element_type=jnp.float32).astype(jnp.bfloat16).reshape(seq_count, kv_local, head_dim)
        q_every = lax.all_gather(q_local, 'ctx', axis=0, tiled=True)
        s_pre = jnp.einsum('bkgd,pkd->bkgp', q_every, k_prefix, preferred_element_type=jnp.float32) * score_scale
        m_pre = jnp.max(s_pre, axis=-1)
        e_pre = jnp.exp(s_pre - m_pre[..., None])
        l_pre = jnp.sum(e_pre, axis=-1)
        o_pre = jnp.einsum('bkgp,pkd->bkgd', e_pre.astype(jnp.bfloat16), v_prefix, preferred_element_type=jnp.float32)
        partial_state = jnp.concatenate([o_pre / l_pre[..., None], (m_pre + jnp.log(l_pre))[..., None]], axis=-1)
        returned = lax.all_to_all(partial_state, 'ctx', 0, 0, tiled=True)
        returned = returned.reshape(ctx_size, seq_count, kv_local, group_size, head_dim + 1)
        o_parts = returned[..., :head_dim]
        lse_parts = returned[..., head_dim]
        slot_ids = jnp.arange(k_suffix.shape[1])
        in_cache = (slot_ids[None, :] < seq_lens[:, None])[:, None, None, :]
        s_cache = jnp.einsum('bkgd,bskd->bkgs', q_local, k_suffix, preferred_element_type=jnp.float32) * score_scale
        s_cache = jnp.where(in_cache, s_cache, -jnp.inf)
        s_self = jnp.einsum('clhe,cle->clh', q_local, k_new, preferred_element_type=jnp.float32) * score_scale
        m_suf = jnp.maximum(jnp.max(s_cache, axis=-1), s_self)
        e_cache = jnp.exp(s_cache - m_suf[..., None])
        e_self = jnp.exp(s_self - m_suf)
        l_suf = jnp.sum(e_cache, axis=-1) + e_self
        o_suf = jnp.einsum('bkgs,bskd->bkgd', e_cache.astype(jnp.bfloat16), v_suffix, preferred_element_type=jnp.float32)
        o_suf = (o_suf + e_self[..., None] * v_new[:, :, None, :].astype(jnp.float32)) / l_suf[..., None]
        lse_suf = m_suf + jnp.log(l_suf)
        lse_max = jnp.maximum(jnp.max(lse_parts, axis=0), lse_suf)
        w_parts = jnp.exp(lse_parts - lse_max)
        w_suf = jnp.exp(lse_suf - lse_max)
        merged = jnp.sum(w_parts[..., None] * o_parts, axis=0) + w_suf[..., None] * o_suf
        merged = merged / (jnp.sum(w_parts, axis=0) + w_suf)[..., None]
        attn_out = merged.astype(jnp.bfloat16).reshape(seq_count, kv_local * group_size * head_dim)
        proj_part = jnp.dot(attn_out, w_o, preferred_element_type=jnp.float32)
        out_hidden = hidden.astype(jnp.float32) + lax.psum(proj_part, 'tp')
        return out_hidden.astype(jnp.bfloat16)

    spec_in = (P(row_axes, None), P(None, 'tp'), P(None, 'tp'), P(None, 'tp'), P('tp', None), P(row_axes, 'tp', None), P(row_axes, 'tp', None), P(row_axes, None, 'tp', None), P(row_axes, None, 'tp', None), P(row_axes))
    return jax.shard_map(device_step, mesh=mesh, in_specs=spec_in, out_specs=P(row_axes, None), check_vma=False)
```

profile of v0, /device:TPU:97, one launch (start us, length us, event | category | flops | bytes accessed | tf_op | source)
XLA Modules:
  0.0 465.0 jit_solution(17143140900669981483)
XLA Ops:
  6.5 0.0 copy-start
  6.6 0.0 all-gather.2.cloned.1.call-start
  6.6 15.7 %fusion.19 = bf16[16,8,16,128]{3,1,2,0:T(8,128)(2,1)S(1)} fusion(bf16[128,8192]{1,0:T(8,128)(2,1)} %param.10, bf16[8192,2048]{1,0:T(8,128)(2,1)} %param.11), kind=kOutput, calls=%fused_computation.23 | convolution fusion | flops 4295229440 | bytes 36175872 | tf_op jit(solution)/shard_map/dot_general | solution.py:17
  22.3 0.1 copy.71
  22.4 0.9 copy.42
  23.3 0.1 all-gather.2.cloned.1.call-update
  23.4 33.7 %all-gather.2.cloned.1.call-done = bf16[1024,2,8,128]{3,0,2,1:T(8,128)(2,1)} async-done(((bf16[128,2,8,128]{3,0,2,1:T(8,128)(2,1)}), bf16[1024,2,8,128]{3,0,2,1:T(8,128)(2,1)}) %all-gather.2.cloned.1.call-update) | async-done | bytes 4194320 | tf_op jit(solution)/shard_map/all_gather | solution.py:21
  57.1 0.0 copy-done
  57.1 10.3 %bitcast_reduce_fusion = (f32[1024,2,8]{0,2,1:T(8,128)S(1)}, f32[2,1024,8,256]{1,3,2,0:T(8,128)}) fusion(bf16[1024,2,8,128]{3,0,2,1:T(8,128)(2,1)} %all-gather.2.cloned.1.call-done, bf16[256,2,128,1]{2,1,0,3:T(2,128)(2,1)S(1)} %bitcast.54), kind=kOutput, calls=%fused_computation.1 | convolution fusion | flops 1082114048 | bytes 21168128 | tf_op jit(solution)/shard_map/bkgd,pkd->bkgp/dot_general | solution.py:22
  67.4 0.0 copy-start.4
  67.4 8.7 %fusion.5 = f32[1024,2,8]{0,2,1:T(8,128)S(1)} fusion(f32[2,1024,8,256]{1,3,2,0:T(8,128)} %get-tuple-element.13, f32[1024,2,8]{0,2,1:T(8,128)S(1)} %get-tuple-element.12), kind=kLoop, calls=%fused_computation.7 | loop fusion | flops 12566528 | bytes 16908288 | tf_op jit(solution)/shard_map/reduce_sum | solution.py:25
  76.1 0.0 copy-done.4
  76.1 7.8 %bitcast_divide_fusion = f32[1024,2,8,128]{0,3,2,1:T(8,128)S(1)} fusion(f32[1024,2,8]{0,2,1:T(8,128)S(1)} %fusion.5, f32[2,1024,8,256]{1,3,2,0:T(8,128)} %get-tuple-element.13, f32[1024,2,8]{0,2,1:T(8,128)S(1)} %get-tuple-element.12, bf16[256,2,128,1]{2,1,0,3:T(2,128)(2,1)S(1)} %bitcast.59), kind=kOutput, calls=%fused_computation.11 | convolution fusion | flops 1088421888 | bytes 25427968 | tf_op jit(solution)/shard_map/bkgp,pkd->bkgd/dot_general | solution.py:26
  84.0 4.4 pad_maximum_fusion
  88.3 17.7 %copy.46 = f32[1024,2,8,129]{3,2,1,0:T(8,128)} copy(f32[1024,2,8,129]{0,3,2,1:T(8,128)} %pad_maximum_fusion) | data formatting | bytes 16908288 | tf_op jit(solution)/shard_map/concatenate | solution.py:27
  106.1 0.0 copy-start.3
  106.1 6.0 %all-to-all-start = ((f32[1024,2,8,129]{3,2,1,0:T(8,128)}), f32[1024,2,8,129]{3,2,1,0:T(8,128)}, u32[]{:S(2)}, u32[]{:S(2)}) async-start(f32[1024,2,8,129]{3,2,1,0:T(8,128)} %copy.46), calls=%async_computation | async-start | bytes 33554432 | tf_op jit(solution)/shard_map/all_to_all | solution.py:28
  112.1 0.0 all-reduce.2.cloned.1.call-start
  112.1 0.0 copy-done.3
  112.1 0.1 iota_compare_fusion
  112.2 0.0 copy-start.2
  112.2 11.7 %fusion.13 = (f32[128,2,8]{2,1,0:T(2,128)S(1)}, f32[128,2,8,256]{3,2,1,0:T(8,128)}) fusion(pred[128,256]{1,0:T(8,128)(4,1)S(1)} %iota_compare_fusion, bf16[128,2,8,128]{3,2,1,0:T(8,128)(2,1)S(1)} %bitcast.56, bf16[128,256,2,128]{3,2,1,0:T(2,128)(2,1)} %param.17), kind=kOutput, calls=%fused_computation.19 | convolution fusion | flops 135788544 | bytes 19439616 | tf_op jit(solution)/shard_map/bkgd,bskd->bkgs/dot_general | solution.py:34
  124.0 0.1 copy.49
  124.0 0.0 copy-done.2
  124.0 2.9 convolution_convert_fusion.2
  127.0 0.4 fusion.59
  127.4 0.1 copy.62
  127.5 0.2 copy.50
  127.7 2.5 fusion.15
  130.1 0.1 copy.51
  130.2 2.9 fusion.20
  133.1 0.7 reshape.66
  133.8 161.8 %all-to-all-done = f32[1024,2,8,129]{3,2,1,0:T(8,128)} async-done(((f32[1024,2,8,129]{3,2,1,0:T(8,128)}), f32[1024,2,8,129]{3,2,1,0:T(8,128)}, u32[]{:S(2)}, u32[]{:S(2)}) %all-to-all-start) | async-done | bytes 8454176 | tf_op jit(solution)/shard_map/all_to_all | solution.py:28
  295.6 7.5 %slice_reduce_fusion = (f32[128,2,8]{2,1,0:T(2,128)S(1)}, f32[8,128,2,8,1]{4,3,2,1,0:T(8,128)}) fusion(f32[8,128,2,8,129]{4,3,2,1,0:T(8,128)} %bitcast.4), kind=kLoop, calls=%fused_computation.56 | loop fusion | flops 14336 | bytes 139264 | tf_op jit(solution)/shard_map/reduce_max | solution.py:44
  303.2 0.1 copy.70
  303.2 4.9 %copy.68 = f32[8,128,2,8,1]{1,0,3,4,2:T(8,128)S(1)} copy(f32[8,128,2,8,1]{4,3,2,1,0:T(8,128)} %get-tuple-element.11) | data formatting | bytes 131072
  308.2 7.1 %slice.9 = f32[8,128,2,8,128]{4,3,2,1,0:T(8,128)} slice(f32[8,128,2,8,129]{4,3,2,1,0:T(8,128)} %bitcast.4), slice={[0:8], [0:128], [0:2], [0:8], [0:128]} | slice | bytes 16777216 | tf_op jit(solution)/shard_map/slice | solution.py:30
  315.3 0.8 copy.55
  316.1 0.8 copy.52
  316.9 0.8 copy.57
  317.7 14.4 %copy.69 = f32[8,128,2,8,128]{1,0,3,4,2:T(8,128)} copy(f32[8,128,2,8,128]{4,3,2,1,0:T(8,128)} %slice.9) | data formatting | bytes 16777216
  332.1 6.4 %multiply_reduce_fusion = f32[128,2,8,128]{0,2,3,1:T(8,128)S(1)} fusion(f32[8,128,2,8,128]{1,0,3,4,2:T(8,128)} %copy.69, f32[8,128,2,8]{1,0,3,2:T(8,128)S(1)} %exponential_bitcast_fusion), kind=kLoop, calls=%fused_computation.12 | loop fusion | flops 3932160 | bytes 9502720 | tf_op jit(solution)/shard_map/reduce_sum | solution.py:47
  338.5 1.5 copy.56
  340.0 0.1 copy.54
  340.2 9.3 %divide_convert_fusion = bf16[128,2,8,128]{3,2,1,0:T(8,128)(2,1)S(1)} fusion(f32[128,2,8,128]{3,2,1,0:T(8,128)} %copy.56, bf16[128,256,2,128]{3,2,1,0:T(2,128)(2,1)} %param.18, f32[128,2,8,256]{3,2,1,0:T(8,128)} %get-tuple-element.15, f32[128,2,8]{2,1,0:T(2,128)S(1)} %copy.50, pred[128,256]{1,0:T(8,128)(4,1)S(1)} %iota_compare_fusion, ...), kind=kOutput, calls=%fused_computation.30 | convolution fusion | flops 138149888 | bytes 20652032 | tf_op jit(solution)/shard_map/bkgs,bskd->bkgd/dot_general | solution.py:41
  349.5 0.0 copy-start.1
  349.5 17.1 %fusion.45 = f32[128,8192]{1,0:T(8,128)} fusion(bf16[2048,8192]{1,0:T(8,128)(2,1)} %param.14, bf16[16,8,16,128]{3,2,1,0:T(8,128)(2,1)S(1)} %bitcast.58), kind=kOutput, calls=%fused_computation.35 | convolution fusion | flops 4294967296 | bytes 38273024 | tf_op jit(solution)/shard_map/dot_general | solution.py:50
  366.5 0.1 all-reduce.2.cloned.1.call-update
  366.6 87.2 %all-reduce.2.cloned.1.call-done = f32[128,8192]{1,0:T(8,128)} async-done(((f32[128,8192]{1,0:T(8,128)}), f32[128,8192]{1,0:T(8,128)}) %all-reduce.2.cloned.1.call-update) | async-done | bytes 4194320 | tf_op jit(solution)/shard_map/psum | solution.py:51
  453.8 3.9 add_convert_fusion
  457.7 0.0 copy-done.1
  (8 shorter events, 0.2 us)
Async XLA Ops:
  6.5 50.6 %copy-start = (bf16[256,2,128]{2,1,0:T(2,128)(2,1)S(1)}, bf16[256,2,128]{2,1,0:T(2,128)(2,1)}, u32[]{:S(2)}) copy-start(bf16[256,2,128]{2,1,0:T(2,128)(2,1)} %param.15) | copy-start | bytes 393220
  6.6 50.6 %all-gather.2.cloned.1.call-start = ((), (), s32[]{:S(2)}) async-start(), calls=%async_computation.1 | async-start | bytes 4718592 | tf_op jit(solution)/shard_map/all_gather | solution.py:21
  67.4 8.7 %copy-start.4 = (bf16[256,2,128]{2,1,0:T(2,128)(2,1)S(1)}, bf16[256,2,128]{2,1,0:T(2,128)(2,1)}, u32[]{:S(2)}) copy-start(bf16[256,2,128]{2,1,0:T(2,128)(2,1)} %param.16) | copy-start | bytes 393220
  106.1 6.1 %copy-start.3 = (s32[128]{0:T(128)S(1)}, s32[128]{0:T(128)}, u32[]{:S(2)}) copy-start(s32[128]{0:T(128)} %param.19) | copy-start | bytes 1540
  106.1 189.5 %all-to-all-start = ((f32[1024,2,8,129]{3,2,1,0:T(8,128)}), f32[1024,2,8,129]{3,2,1,0:T(8,128)}, u32[]{:S(2)}, u32[]{:S(2)}) async-start(f32[1024,2,8,129]{3,2,1,0:T(8,128)} %copy.46), calls=%async_computation | async-start | bytes 33554432 | tf_op jit(solution)/shard_map/all_to_all | solution.py:28
  112.1 341.7 %all-reduce.2.cloned.1.call-start = ((), (), s32[]{:S(2)}) async-start(), calls=%async_computation.2 | async-start | bytes 8388608 | tf_op jit(solution)/shard_map/psum | solution.py:51
  112.2 11.8 %copy-start.2 = (bf16[128,8192]{1,0:T(8,128)(2,1)S(1)}, bf16[128,8192]{1,0:T(8,128)(2,1)}, u32[]{:S(2)}) copy-start(bf16[128,8192]{1,0:T(8,128)(2,1)} %param.10) | copy-start | bytes 6291460
  349.5 108.3 %copy-start.1 = (bf16[256,2,128]{2,1,0:T(2,128)(2,1)S(1)}, bf16[256,2,128]{2,1,0:T(2,128)(2,1)}, u32[]{:S(2)}) copy-start(bf16[256,2,128]{2,1,0:T(2,128)(2,1)} %param.15) | copy-start | bytes 393220
Sparse Core Ops, SparseCore 0:
  23.5 33.5 all-gather.1
  366.7 87.0 all-reduce.1
where the time goes:
time: 473 us; the launch traced here: 465 us
  waiting for transfers between devices  283 us (60%)
  matrix products  78.1 us (17%)
  local copies, waits for them, and re-layouts  50.4 us (11%)
  other arithmetic  33.6 us (7%)
  between operations  14 us (3%)
  starting transfers between devices  6.05 us (1%)
    all_to_all x1, waiting for transfers between devices, device_step(): returned = lax.all_to_all(partial_state, 'ctx', 0, 0, tiled=True)  162 us
    psum x1, waiting for transfers between devices, device_step(): out_hidden = hidden.astype(jnp.float32) + lax.psum(proj_part, 'tp')  87.2 us
    all_gather x1, waiting for transfers between devices, device_step(): q_every = lax.all_gather(q_local, 'ctx', axis=0, tiled=True)  33.7 us
    unnamed x14, local copies, waits for them, and re-layouts  19.4 us
    concatenate x1, local copies, waits for them, and re-layouts, device_step(): jnp.concatenate([o_pre / l_pre[..., None], (m_pre + jnp.log(l_pre))[...,...  17.7 us
    dot_general x1, matrix products, device_step(): proj_part = jnp.dot(attn_out, w_o, preferred_element_type=jnp.float32)  17.1 us
    dot_general x1, matrix products, device_step(): jnp.dot(hidden, w_q, preferred_element_type=jnp.float32)  15.7 us
    dot_general x1, matrix products, device_step(): jnp.einsum('bkgd,bskd->bkgs', q_local, k_suffix, preferred_element_type=j...  11.7 us
  transfers between devices with their start and end apart: 3, of which 3 were waited for; matrix products, arithmetic and copies ran while one was open for 5% of the time, Pallas kernels for 0%

commit v1 on v0

v1 whole, which is shorter than its diff:
```python
import functools
import math

import jax
import jax.numpy as jnp
from jax import lax
from jax.experimental import pallas as pl
from jax.experimental.pallas import tpu as pltpu
from jax.sharding import PartitionSpec as P

MESH = pl.DeviceIdType.MESH
F32, BF16 = jnp.float32, jnp.bfloat16


def qkv_gather_kernel(x_ref, kvp_ref, wq_ref, wk_ref, wv_ref, qkv_ref, all_ref, wbuf, wsem, send_sem, recv_sem, pair_send, pair_recv):
    n_ctx = all_ref.shape[0]
    me = lax.axis_index('ctx')
    right, left = lax.rem(me + 2, n_ctx), lax.rem(me + n_ctx - 2, n_ctx)
    far = lax.rem(me + 4, n_ctx)
    partner = me + 1 - 2 * lax.rem(me, 2)
    depth, width = wk_ref.shape
    q_blocks = wq_ref.shape[1] // width
    blocks = q_blocks + 2
    bufs = wbuf.shape[0]

    def fetch(j):
        slot = lax.rem(j, bufs)

        @pl.when(j < q_blocks)
        def _():
            columns = pl.ds(pl.multiple_of(j * width, width), width)
            pltpu.make_async_copy(wq_ref.at[:, columns], wbuf.at[slot], wsem.at[slot]).start()

        @pl.when(j == q_blocks)
        def _():
            pltpu.make_async_copy(wk_ref, wbuf.at[slot], wsem.at[slot]).start()

        @pl.when(j == q_blocks + 1)
        def _():
            pltpu.make_async_copy(wv_ref, wbuf.at[slot], wsem.at[slot]).start()

    for j in range(bufs):
        fetch(jnp.int32(j))

    barrier = pltpu.get_barrier_semaphore()
    for peer in (left, right, partner):
        pl.semaphore_signal(barrier, inc=1, device_id={'ctx': peer}, device_id_type=MESH)
    pl.semaphore_wait(barrier, 3)

    def send(src, dst, index, peer):
        return pltpu.make_async_remote_copy(src_ref=src, dst_ref=dst, send_sem=send_sem.at[index], recv_sem=recv_sem.at[index], device_id={'ctx': peer}, device_id_type=MESH)

    def to_partner(slot, index):
        src = kvp_ref if slot is None else all_ref.at[slot]
        dst = all_ref.at[me if slot is None else slot]
        return pltpu.make_async_remote_copy(src_ref=src, dst_ref=dst, send_sem=pair_send.at[index], recv_sem=pair_recv.at[index], device_id={'ctx': partner}, device_id_type=MESH)

    go_right = send(kvp_ref, all_ref.at[me], 0, right)
    go_left = send(kvp_ref, all_ref.at[me], 1, left)
    go_right.start()
    go_left.start()
    own_pair = to_partner(None, 0)
    own_pair.start()
    all_ref[me] = kvp_ref[...]

    def project(j, carry):
        slot = lax.rem(j, bufs)
        pltpu.make_async_copy(wk_ref, wbuf.at[slot], wsem.at[slot]).wait()
        qkv_ref[j] = jnp.dot(x_ref[...], wbuf[slot], preferred_element_type=F32).astype(BF16)
        fetch(j + bufs)
        return carry

    split = min(7, blocks - 2)
    lax.fori_loop(0, split, project, 0)

    send(kvp_ref, all_ref.at[left], 0, right).wait_recv()
    on_right = send(all_ref.at[left, 0], all_ref.at[left, 0], 2, right)
    on_right.start()
    send(kvp_ref, all_ref.at[right], 1, left).wait_recv()
    on_left = send(all_ref.at[right, 1], all_ref.at[right, 1], 3, left)
    on_left.start()
    left_pair = to_partner(left, 1)
    left_pair.start()
    right_pair = to_partner(right, 2)
    right_pair.start()

    lax.fori_loop(split, blocks, project, 0)

    send(all_ref.at[far, 0], all_ref.at[far, 0], 2, right).wait_recv()
    send(all_ref.at[far, 1], all_ref.at[far, 1], 3, left).wait_recv()
    far_pair = to_partner(far, 3)
    far_pair.start()
    for copy in (go_right, go_left, on_right, on_left):
        copy.wait_send()
    for copy in (own_pair, left_pair, right_pair, far_pair):
        copy.wait_send()
    shift = partner - me
    for index, slot in enumerate((me, left, right, far)):
        landed = all_ref.at[slot + shift]
        pltpu.make_async_remote_copy(src_ref=landed, dst_ref=landed, send_sem=pair_send.at[index], recv_sem=pair_recv.at[index], device_id={'ctx': partner}, device_id_type=MESH).wait_recv()


def attention_kernel(scale, len_ref, qa_ref, kn_ref, vn_ref, qb_ref, ks_ref, vs_ref, kvp_ref, out_ref, o_suf, m_suf, l_suf):
    seqs, kv_heads, group, dim = out_ref.shape
    rows = kv_heads * group
    slots = ks_ref.shape[1]
    first = pl.program_id(0) * seqs
    sub = min(8, seqs)
    factor = scale * math.log2(math.e)
    dims = (((1,), (1,)), ((), ()))

    column = lax.broadcasted_iota(jnp.int32, (rows, slots), 1)
    head = lax.broadcasted_iota(jnp.int32, (rows, slots), 0) // group
    place = jnp.where(lax.rem(column, kv_heads) == head, column // kv_heads, slots)

    def suffix(i, carry):
        span = pl.ds(pl.multiple_of(i * sub * rows, sub * rows), sub * rows)
        scores = []
        for s in range(sub):
            q_one = qa_ref[pl.ds(pl.multiple_of((i * sub + s) * rows, rows), rows)]
            one = lax.dot_general(q_one, ks_ref[i * sub + s], dims, preferred_element_type=F32)
            scores.append(jnp.where(place < len_ref[first + i * sub + s], one, -jnp.inf))
        scores = jnp.concatenate(scores, axis=0)
        own = jnp.sum(qa_ref[span].astype(F32) * kn_ref[span].astype(F32), axis=-1, keepdims=True)
        top = jnp.maximum(jnp.max(scores, axis=-1, keepdims=True), own)
        e = jnp.exp2((scores - top) * factor)
        e_own = jnp.exp2((own - top) * factor)
        total = jnp.sum(e, axis=-1, keepdims=True) + e_own
        e = e.astype(BF16)
        o = [jnp.dot(e[s * rows:(s + 1) * rows], vs_ref[i * sub + s], preferred_element_type=F32) for s in range(sub)]
        o = jnp.concatenate(o, axis=0) + e_own * vn_ref[span].astype(F32)
        block = pl.ds(i * sub, sub)
        o_suf[block] = o.reshape(sub, kv_heads, group, dim)
        m_suf[block] = top.reshape(sub, kv_heads, group, 1)
        l_suf[block] = total.reshape(sub, kv_heads, group, 1)
        return carry

    lax.fori_loop(0, seqs // sub, suffix, 0)

    for kv in range(kv_heads):
        keys = kvp_ref[:, 0, kv].reshape(-1, dim)
        values = kvp_ref[:, 1, kv].reshape(-1, dim)
        s = lax.dot_general(qb_ref[kv], keys, dims, preferred_element_type=F32)
        top_pre = jnp.max(s, axis=-1, keepdims=True)
        e = jnp.exp2((s - top_pre) * factor)
        total_pre = jnp.sum(e, axis=-1, keepdims=True)
        o_pre = jnp.dot(e.astype(BF16), values, preferred_element_type=F32)
        top_suf = m_suf[:, kv].reshape(seqs * group, 1)
        top = jnp.maximum(top_pre, top_suf)
        w_pre = jnp.exp2((top_pre - top) * factor)
        w_suf = jnp.exp2((top_suf - top) * factor)
        total = w_pre * total_pre + w_suf * l_suf[:, kv].reshape(seqs * group, 1)
        o = (w_pre * o_pre + w_suf * o_suf[:, kv].reshape(seqs * group, dim)) / total
        out_ref[:, kv] = o.reshape(seqs, group, dim).astype(BF16)


ORDER = ((2, 0), (2, 1), (1, 0), (3, 1), (1, 1), (3, 0), (0, 0), (0, 1))


def project_reduce_kernel(n_tp, pieces, att_ref, x_ref, wo_ref, y_ref, wbuf, part, first_in, direct_in, sum_in, wsem, send_sem, recv_sem):
    me = lax.axis_index('tp')
    right, left = lax.rem(me + 1, n_tp), lax.rem(me + n_tp - 1, n_tp)
    rows = att_ref.shape[0]
    half = wbuf.shape[2]
    bufs = wbuf.shape[0]
    step = rows // pieces

    def columns(owner, which, width):
        return pl.ds(pl.multiple_of((owner * 2 + which) * half, half), width)

    def weights(k):
        away, which = ORDER[k]
        return pltpu.make_async_copy(wo_ref.at[:, columns(lax.rem(me + away, n_tp), which, half)], wbuf.at[k % bufs], wsem.at[k % bufs])

    for k in range(bufs):
        weights(k).start()

    barrier = pltpu.get_barrier_semaphore()
    for peer in (left, right):
        pl.semaphore_signal(barrier, inc=1, device_id={'tp': peer}, device_id_type=MESH)
    pl.semaphore_wait(barrier, 2)

    def copy(kind, way, p, src, dst):
        return pltpu.make_async_remote_copy(src_ref=src, dst_ref=dst, send_sem=send_sem.at[kind, way, p], recv_sem=recv_sem.at[kind, way, p], device_id={'tp': (right, left)[way]}, device_id_type=MESH)

    def span(p):
        return pl.ds(p * step, step)

    started = []

    def launch(*args):
        one = copy(*args)
        one.start()
        started.append(one)

    def compute(k):
        weights(k).wait()
        part[k] = jnp.dot(att_ref[...], wbuf[k % bufs], preferred_element_type=F32)
        if k + bufs < len(ORDER):
            weights(k + bufs).start()

    compute(0)
    for p in range(pieces):
        launch(0, 1, p, part.at[0, span(p)], first_in.at[1, span(p)])
    compute(1)
    for p in range(pieces):
        launch(0, 0, p, part.at[1, span(p)], first_in.at[0, span(p)])
    compute(2)
    for p in range(pieces):
        launch(1, 0, p, part.at[2, span(p)], direct_in.at[0, span(p)])
    compute(3)
    for p in range(pieces):
        launch(1, 1, p, part.at[3, span(p)], direct_in.at[1, span(p)])
    for k in range(4, 8):
        compute(k)
    for p in range(pieces):
        for way, k in ((0, 4), (1, 5)):
            copy(0, way, p, first_in.at[way, span(p)], first_in.at[way, span(p)]).wait_recv()
            part[k, span(p)] += first_in[way, span(p)]
            launch(2, way, p, part.at[k, span(p)], sum_in.at[way, span(p)])
    mine = columns(me, 0, 2 * half)
    for p in range(pieces):
        for way in (0, 1):
            copy(1, way, p, direct_in.at[way, span(p)], direct_in.at[way, span(p)]).wait_recv()
            copy(2, way, p, sum_in.at[way, span(p)], sum_in.at[way, span(p)]).wait_recv()
        for which in (0, 1):
            total = part[6 + which, span(p)] + sum_in[1 - which, span(p)] + direct_in[which, span(p)]
            total = total + x_ref[span(p), columns(me, which, half)].astype(F32)
            y_ref[span(p), columns(me, which, half)] = total.astype(BF16)
        for way in (0, 1):
            launch(3, way, p, y_ref.at[span(p), mine], y_ref.at[span(p), mine])
    for p in range(pieces):
        for way, source in ((0, left), (1, right)):
            block = y_ref.at[span(p), columns(source, 0, 2 * half)]
            copy(3, way, p, block, block).wait_recv()
            block = y_ref.at[span(p), columns(source, way, half)]
            launch(4, way, p, block, block)
    far = lax.rem(me + 2, n_tp)
    for p in range(pieces):
        for way in (0, 1):
            block = y_ref.at[span(p), columns(far, way, half)]
            copy(4, way, p, block, block).wait_recv()
    for one in started:
        one.wait_send()


def solution(mesh):
    n_ctx, n_tp = mesh.shape['ctx'], mesh.shape['tp']
    row_axes = ('dp', 'ctx')
    vmem = pl.BlockSpec(memory_space=pltpu.VMEM)
    hbm = pl.BlockSpec(memory_space=pl.ANY)
    limit = 60 * 1024 * 1024

    def device_step(hidden, w_q, w_k, w_v, w_o, k_prefix, v_prefix, k_suffix, v_suffix, seq_lens):
        seqs, model = hidden.shape
        positions, kv_heads, dim = k_prefix.shape
        slots = k_suffix.shape[1]
        group = w_q.shape[1] // (kv_heads * dim)
        heads = kv_heads * group
        width = w_k.shape[1]
        blocks = w_q.shape[1] // width + 2

        kv_own = jnp.stack([k_prefix, v_prefix]).transpose(0, 2, 1, 3)
        qkv, kv_all = pl.pallas_call(
            qkv_gather_kernel,
            name='qkv_gather',
            out_shape=(jax.ShapeDtypeStruct((blocks, seqs, width), BF16), jax.ShapeDtypeStruct((n_ctx, 2, kv_heads, positions, dim), BF16)),
            in_specs=[vmem, vmem, hbm, hbm, hbm],
            out_specs=(vmem, vmem),
            scratch_shapes=[pltpu.VMEM((4, model, width), BF16), pltpu.SemaphoreType.DMA((4,)), pltpu.SemaphoreType.DMA((4,)), pltpu.SemaphoreType.DMA((4,)), pltpu.SemaphoreType.DMA((4,)), pltpu.SemaphoreType.DMA((4,))],
            compiler_params=pltpu.CompilerParams(collective_id=0, has_side_effects=True, vmem_limit_bytes=limit),
        )(hidden, kv_own, w_q, w_k, w_v)

        per = width // dim
        q = qkv[:blocks - 2].reshape(blocks - 2, seqs, per, dim)
        q_rows = q.transpose(1, 0, 2, 3).reshape(seqs * heads, dim)
        q_heads = q_rows.reshape(seqs, kv_heads, group, dim).transpose(1, 0, 2, 3).reshape(kv_heads, seqs * group, dim)
        k_new, v_new = (jnp.broadcast_to(a.reshape(seqs, kv_heads, 1, dim), (seqs, kv_heads, group, dim)).reshape(seqs * heads, dim) for a in (qkv[blocks - 2], qkv[blocks - 1]))

        nb = min(32, seqs)
        row_spec = pl.BlockSpec((nb * heads, dim), lambda i, lens: (i, 0))
        cache_spec = pl.BlockSpec((nb, slots * kv_heads, dim), lambda i, lens: (i, 0, 0))
        att = pl.pallas_call(
            functools.partial(attention_kernel, dim ** -0.5),
            name='attention',
            out_shape=jax.ShapeDtypeStruct((seqs, kv_heads, group, dim), BF16),
            grid_spec=pltpu.PrefetchScalarGridSpec(
                num_scalar_prefetch=1,
                grid=(seqs // nb,),
                in_specs=[row_spec, row_spec, row_spec, pl.BlockSpec((kv_heads, nb * group, dim), lambda i, lens: (0, i, 0)), cache_spec, cache_spec, pl.BlockSpec((n_ctx, 2, kv_heads, positions, dim), lambda i, lens: (0, 0, 0, 0, 0))],
                out_specs=pl.BlockSpec((nb, kv_heads, group, dim), lambda i, lens: (i, 0, 0, 0)),
                scratch_shapes=[pltpu.VMEM((nb, kv_heads, group, dim), F32), pltpu.VMEM((nb, kv_heads, group, 1), F32), pltpu.VMEM((nb, kv_heads, group, 1), F32)],
            ),
            compiler_params=pltpu.CompilerParams(vmem_limit_bytes=limit),
        )(seq_lens, q_rows, k_new, v_new, q_heads, k_suffix.reshape(seqs, slots * kv_heads, dim), v_suffix.reshape(seqs, slots * kv_heads, dim), kv_all)
        att = att.reshape(seqs, heads * dim)

        half = model // (2 * n_tp)
        pieces = 4
        return pl.pallas_call(
            functools.partial(project_reduce_kernel, n_tp, pieces),
            name='project_reduce',
            out_shape=jax.ShapeDtypeStruct((seqs, model), BF16),
            in_specs=[vmem, vmem, hbm],
            out_specs=vmem,
            scratch_shapes=[
                pltpu.VMEM((3, heads * dim, half), BF16),
                pltpu.VMEM((8, seqs, half), F32),
                pltpu.VMEM((2, seqs, half), F32),
                pltpu.VMEM((2, seqs, half), F32),
                pltpu.VMEM((2, seqs, half), F32),
                pltpu.SemaphoreType.DMA((3,)),
                pltpu.SemaphoreType.DMA((5, 2, pieces)),
                pltpu.SemaphoreType.DMA((5, 2, pieces)),
            ],
            compiler_params=pltpu.CompilerParams(collective_id=1, has_side_effects=True, vmem_limit_bytes=limit),
        )(att, hidden, w_o)

    spec_in = (P(row_axes, None), P(None, 'tp'), P(None, 'tp'), P(None, 'tp'), P('tp', None), P(row_axes, 'tp', None), P(row_axes, 'tp', None), P(row_axes, None, 'tp', None), P(row_axes, None, 'tp', None), P(row_axes))
    return jax.shard_map(device_step, mesh=mesh, in_specs=spec_in, out_specs=P(row_axes, None), check_vma=False)
```

time: 473 us -> 123 us (0.26); the launches traced: 465 us -> 123 us
  waiting for transfers between devices: 283 us -> 0 us
  Pallas kernels: 0 us -> 110 us
  matrix products: 78.1 us -> 0 us
  local copies, waits for them, and re-layouts: 50.4 us -> 12.5 us
  other arithmetic: 33.6 us -> 0.73 us
  between operations: 14 us -> 0.04 us
  starting transfers between devices: 6.05 us -> 0 us
    all_to_all x1 -> x0, waiting for transfers between devices: 162 us -> none  [device_step(): returned = lax.all_to_all(partial_state, 'ctx', 0, 0, tiled=True)]
    pallas_call x0 -> x3, Pallas kernels: none -> 110 us  [the longest x1 63.9 us: device_step(): pl.pallas_call(functools.partial(project_reduce_kernel, n_tp, pieces), na...]
    psum x1 -> x0, waiting for transfers between devices: 87.2 us -> none  [device_step(): out_hidden = hidden.astype(jnp.float32) + lax.psum(proj_part, 'tp')]
    dot_general x9 -> x0, matrix products: 78.1 us -> none  [the longest x1 17.1 us: device_step(): proj_part = jnp.dot(attn_out, w_o, preferred_element_type=jnp.float32)]
    all_gather x1 -> x0, waiting for transfers between devices: 33.7 us -> none  [device_step(): q_every = lax.all_gather(q_local, 'ctx', axis=0, tiled=True)]
    concatenate x1 -> x0, local copies, waits for them, and re-layouts: 17.7 us -> none  [device_step(): jnp.concatenate([o_pre / l_pre[..., None], (m_pre + jnp.log(l_pre))[...,...]
    reduce_sum x4 -> x0, other arithmetic: 17.6 us -> none  [the longest x1 8.65 us: device_step(): l_pre = jnp.sum(e_pre, axis=-1)]
    unnamed x14 -> x2, local copies, waits for them, and re-layouts: 19.4 us -> 5.07 us
  transfers between devices with their start and end apart: 3 -> 0, of which waited for: 3 -> 0; matrix products, arithmetic and copies ran while one was open for 5% -> 0% of each run, Pallas kernels for 0% -> 0%
where the time goes in v1:
time: 123 us
  Pallas kernels  110 us (89%)
  local copies, waits for them, and re-layouts  12.5 us (10%)
    pallas_call x1, Pallas kernels, device_step(): pl.pallas_call(functools.partial(project_reduce_kernel, n_tp, pieces), na...  63.9 us
    pallas_call x1, Pallas kernels, device_step(): pl.pallas_call(qkv_gather_kernel, name='qkv_gather', out_shape=(jax.Shape...  22.9 us
    pallas_call x1, Pallas kernels, device_step(): pl.pallas_call(functools.partial(attention_kernel, dim ** (-0.5)), name='...  22.8 us
    unnamed x2, local copies, waits for them, and re-layouts  5.07 us

profile of v1, /device:TPU:97, one launch (start us, length us, event | category | flops | bytes accessed | tf_op | source)
XLA Modules:
  0.0 123.0 jit_solution(8827539465775722022)
XLA Ops:
  0.0 1.0 copy_bitcast_fusion.3
  1.0 0.7 maximum_bitcast_fusion.kvp_ref
  1.7 22.9 %qkv_gather.1 = (bf16[10,128,256]{2,1,0:T(8,128)(2,1)}, bf16[8,2,2,256,128]{4,3,2,1,0:T(8,128)(2,1)}) custom-call(bf16[128,8192]{1,0:T(8,128)(2,1)} %x_ref.3, bf16[2,2,256,128]{3,2,1,0:T(8,128)(2,1)} %maximum_bitcast_fusion.kvp_ref, bf16[8192,2048]{1,0:T(8,128)(2,1)} %wq_ref.1, bf16[8192,256]{1,0:T(8,128)(2,1)} %wk_ref.1, bf16[8192,256]{1,0:T(8,128)(2,1)} %wv_ref.1), custom_call_target="tpu_custom_call" | custom-call | tf_op jit(solution)/shard_map/qkv_gather/pallas_call | solution.py:264
  24.7 0.9 fusion.1
  25.6 1.3 %copy_bitcast_fusion.1 = (bf16[8,128,2,128]{3,1,2,0:T(8,128)(2,1)S(1)}, bf16[128,8,2,128]{3,0,2,1:T(8,128)(2,1)S(1)}) fusion(bf16[10,128,256]{2,1,0:T(8,128)(2,1)} %get-tuple-element.7), kind=kLoop, calls=%fused_computation.1 | loop fusion | bytes 1572864 | tf_op jit(solution)/shard_map/reshape | solution.py:275
  26.9 1.1 copy.29
  28.0 0.9 broadcast_in_dim.15
  28.9 0.9 broadcast_in_dim.17
  29.8 1.3 %copy.17 = bf16[128,8,2,128]{3,2,1,0:T(2,128)(2,1)} copy(bf16[128,8,2,128]{3,0,2,1:T(8,128)(2,1)S(1)} %get-tuple-element.12) | data formatting | bytes 1048576 | tf_op jit(solution)/shard_map/transpose | solution.py:276
  31.1 22.8 %attention.1 = bf16[128,2,8,128]{3,2,1,0:T(8,128)(2,1)} custom-call(s32[128]{0:T(128)} %len_ref.1, bf16[2048,128]{1,0:T(8,128)(2,1)} %bitcast.37, bf16[2048,128]{1,0:T(8,128)(2,1)} %bitcast.35, bf16[2048,128]{1,0:T(8,128)(2,1)} %bitcast.36, bf16[2,1024,128]{2,1,0:T(8,128)(2,1)} %bitcast.34, bf16[128,512,128]{2,1,0:T(8,128)(2,1)} %bitcast.32, ...), custom_call_target="tpu_custom_call" | custom-call | tf_op jit(solution)/shard_map/attention/pallas_call | solution.py:283
  54.0 2.0 %copy.28 = bf16[16,8,16,128]{3,1,2,0:T(8,128)(2,1)} copy(bf16[16,8,16,128]{3,2,1,0:T(8,128)(2,1)} %bitcast.38) | data formatting | bytes 1048576
  55.9 63.9 %project_reduce.1 = bf16[128,8192]{1,0:T(8,128)(2,1)} custom-call(bf16[128,2048]{1,0:T(8,128)(2,1)} %bitcast.39, bf16[128,8192]{1,0:T(8,128)(2,1)} %x_ref.3, bf16[2048,8192]{1,0:T(8,128)(2,1)} %wo_ref.1), custom_call_target="tpu_custom_call" | custom-call | tf_op jit(solution)/shard_map/project_reduce/pallas_call | solution.py:300
  119.9 3.1 %copy.31 = bf16[128,8192]{1,0:T(8,128)(2,1)} copy(bf16[128,8192]{1,0:T(8,128)(2,1)} %project_reduce.1) | data formatting | bytes 4194304
  (2 shorter events, 0.0 us)

commit v2 on v0

v2 whole, which is shorter than its diff:
```python
import functools
import math

import jax
import jax.numpy as jnp
from jax import lax
from jax.experimental import pallas as pl
from jax.experimental.pallas import tpu as pltpu
from jax.sharding import PartitionSpec as P

MESH = pl.DeviceIdType.MESH
F32, BF16 = jnp.float32, jnp.bfloat16
LAST = (((1,), (1,)), ((), ()))

ORDER = ((2, 0), (2, 1), (1, 0), (3, 1), (1, 1), (3, 0), (0, 0), (0, 1))
SUB = 8
DEPTH = 3
PREFIX = 32
CHUNKS = 2
PIECES = 4


def layer_kernel(scale, n_ctx, n_tp, len_ref, kp_ref, vp_ref, x_hbm, wq_hbm, wk_hbm, wv_hbm, wo_hbm, ks_hbm, vs_hbm, y_ref,
                 x_ref, pool, kv_all, q_ref, new_ref, kbuf, vbuf, o_suf, m_suf, l_suf, flat, att_ref, part, first_in, direct_in, sum_in,
                 x_sem, wsem, ksem, vsem, ring_send, ring_recv, pair_send, pair_recv, send_sem, recv_sem):
    kv_heads, positions, dim = kv_all.shape[2:]
    seqs = x_ref.shape[0]
    model, width = wk_hbm.shape
    inner = wo_hbm.shape[0]
    group = inner // (kv_heads * dim)
    heads = kv_heads * group
    slots = kbuf.shape[2]
    q_blocks = inner // width
    blocks = q_blocks + 2
    bufs = pool.shape[0]
    half = part.shape[2]
    tiles = half // width
    rows = seqs // CHUNKS
    step = seqs // PIECES
    per = PIECES // CHUNKS
    factor = scale * math.log2(math.e)

    here = lax.axis_index('ctx')
    x_right, x_left, x_far = lax.rem(here + 2, n_ctx), lax.rem(here + n_ctx - 2, n_ctx), lax.rem(here + 4, n_ctx)
    partner = here + 1 - 2 * lax.rem(here, 2)
    me = lax.axis_index('tp')
    right, left, far = lax.rem(me + 1, n_tp), lax.rem(me + n_tp - 1, n_tp), lax.rem(me + 2, n_tp)

    def columns(owner, which, size):
        return pl.ds(pl.multiple_of((owner * 2 + which) * half, half), size)

    def fetch_q(j, slot):
        where = pl.ds(pl.multiple_of(j * width, width), width)
        return pltpu.make_async_copy(wq_hbm.at[:, where], pool.at[slot], wsem.at[slot])

    def fetch_o(k, slot):
        away = sum(jnp.where(k == n, ORDER[n][0], 0) for n in range(8))
        which = sum(jnp.where(k == n, ORDER[n][1], 0) for n in range(8))
        start = (lax.rem(me + away, n_tp) * 2 + which) * half
        for t in range(tiles):
            where = pl.ds(pl.multiple_of(start + t * width, width), width)
            pltpu.make_async_copy(wo_hbm.at[:, where], pool.at[slot, pl.ds(t * inner, inner)], wsem.at[slot]).start()

    def weights_here(slot):
        pltpu.make_async_copy(wk_hbm, pool.at[slot], wsem.at[slot]).wait()

    def fetch_suffix(g):
        slot = lax.rem(g, DEPTH)
        which = pl.ds(g * SUB, SUB)
        return (pltpu.make_async_copy(ks_hbm.at[which], kbuf.at[slot], ksem.at[slot]),
                pltpu.make_async_copy(vs_hbm.at[which], vbuf.at[slot], vsem.at[slot]))

    x_copy = pltpu.make_async_copy(x_hbm, x_ref, x_sem)
    x_copy.start()
    for j in range(bufs):
        fetch_q(j, j).start()

    barrier = pltpu.get_barrier_semaphore()
    for axis, peer in (('ctx', x_left), ('ctx', x_right), ('ctx', partner), ('tp', left), ('tp', right)):
        pl.semaphore_signal(barrier, inc=1, device_id={axis: peer}, device_id_type=MESH)

    pick_row = lax.broadcasted_iota(jnp.int32, (positions, positions * kv_heads), 0)
    pick_col = lax.broadcasted_iota(jnp.int32, (positions, positions * kv_heads), 1)
    for kv in range(kv_heads):
        pick = jnp.where(pick_col == pick_row * kv_heads + kv, 1.0, 0.0).astype(BF16)
        for n, ref in enumerate((kp_ref, vp_ref)):
            kv_all[here, n, kv] = jnp.dot(pick, ref[...], preferred_element_type=F32).astype(BF16)
    pl.semaphore_wait(barrier, 5)

    def ring(src, dst, index, peer):
        return pltpu.make_async_remote_copy(src_ref=src, dst_ref=dst, send_sem=ring_send.at[index], recv_sem=ring_recv.at[index], device_id={'ctx': peer}, device_id_type=MESH)

    def pair(slot, index):
        block = kv_all.at[slot]
        return pltpu.make_async_remote_copy(src_ref=block, dst_ref=block, send_sem=pair_send.at[index], recv_sem=pair_recv.at[index], device_id={'ctx': partner}, device_id_type=MESH)

    own = kv_all.at[here]
    ring(own, own, 0, x_right).start()
    ring(own, own, 1, x_left).start()
    pair(here, 0).start()
    x_copy.wait()

    def project_in(j, carry):
        slot = lax.rem(j, bufs)
        weights_here(slot)
        block = jnp.dot(x_ref[...], pool[slot], preferred_element_type=F32).astype(BF16).astype(F32)
        per_block = width // dim

        @pl.when(j < q_blocks)
        def _():
            for i in range(per_block):
                head = j * per_block + i
                q_ref[head // group, pl.ds(lax.rem(head, group), seqs, stride=group), :] = block[:, i * dim:(i + 1) * dim]

        @pl.when(j >= q_blocks)
        def _():
            for i in range(per_block):
                new_ref[j - q_blocks, i] = block[:, i * dim:(i + 1) * dim]

        @pl.when(j + bufs < q_blocks)
        def _():
            fetch_q(j + bufs, slot).start()

        @pl.when(j + bufs == q_blocks)
        def _():
            pltpu.make_async_copy(wk_hbm, pool.at[slot], wsem.at[slot]).start()

        @pl.when(j + bufs == q_blocks + 1)
        def _():
            pltpu.make_async_copy(wv_hbm, pool.at[slot], wsem.at[slot]).start()

        @pl.when(j == 1)
        def _():
            for g in range(min(DEPTH, seqs // SUB)):
                for copy in fetch_suffix(jnp.int32(g)):
                    copy.start()

        @pl.when(j >= blocks - bufs)
        def _():
            fetch_o(j - (blocks - bufs), slot)

        @pl.when(j == blocks - 4)
        def _():
            ring(kv_all.at[x_left], kv_all.at[x_left], 0, x_right).wait_recv()
            ring(kv_all.at[x_left, 0], kv_all.at[x_left, 0], 2, x_right).start()
            ring(kv_all.at[x_right], kv_all.at[x_right], 1, x_left).wait_recv()
            ring(kv_all.at[x_right, 1], kv_all.at[x_right, 1], 3, x_left).start()
            pair(x_left, 1).start()
            pair(x_right, 2).start()

        return carry

    lax.fori_loop(0, blocks, project_in, 0)

    ring(kv_all.at[x_far, 0], kv_all.at[x_far, 0], 2, x_right).wait_recv()
    ring(kv_all.at[x_far, 1], kv_all.at[x_far, 1], 3, x_left).wait_recv()
    pair(x_far, 3).start()

    column = lax.broadcasted_iota(jnp.int32, (heads, slots), 1)
    head_of = lax.broadcasted_iota(jnp.int32, (heads, slots), 0) // group
    place = jnp.where(lax.rem(column, kv_heads) == head_of, column // kv_heads, slots)

    def suffix(g, chunk):
        slot = lax.rem(g, DEPTH)
        for copy in fetch_suffix(g):
            copy.wait()
        base = pl.multiple_of(g * SUB, SUB)
        new = [[new_ref[n, kv, pl.ds(base, SUB)] for kv in range(kv_heads)] for n in range(2)]
        spread = [jnp.concatenate([jnp.broadcast_to(new[n][kv][s:s + 1], (group, dim)) for s in range(SUB) for kv in range(kv_heads)], axis=0) for n in range(2)]
        q_blk = [q_ref[kv, pl.ds(pl.multiple_of(base * group, SUB * group), SUB * group)] for kv in range(kv_heads)]
        q_all = jnp.concatenate([q_blk[kv][s * group:(s + 1) * group] for s in range(SUB) for kv in range(kv_heads)], axis=0)
        q_low = q_all.astype(BF16)
        scores = []
        for s in range(SUB):
            one = lax.dot_general(q_low[s * heads:(s + 1) * heads], kbuf[slot, s], LAST, preferred_element_type=F32)
            scores.append(jnp.where(place < len_ref[base + s], one, -jnp.inf))
        scores = jnp.concatenate(scores, axis=0)
        own_score = jnp.sum(q_all * spread[0], axis=-1, keepdims=True)
        top = jnp.maximum(jnp.max(scores, axis=-1, keepdims=True), own_score)
        e = jnp.exp2((scores - top) * factor)
        e_own = jnp.exp2((own_score - top) * factor)
        total = jnp.sum(e, axis=-1, keepdims=True) + e_own
        e = e.astype(BF16)
        o = [jnp.dot(e[s * heads:(s + 1) * heads], vbuf[slot, s], preferred_element_type=F32) for s in range(SUB)]
        o = jnp.concatenate(o, axis=0) + e_own * spread[1]
        for s in range(SUB):
            for kv in range(kv_heads):
                src = slice(s * heads + kv * group, s * heads + (kv + 1) * group)
                dst = pl.ds(pl.multiple_of((base - chunk * rows + s) * group, group), group)
                o_suf[kv, dst] = o[src]
                m_suf[kv, dst] = top[src]
                l_suf[kv, dst] = total[src]

        @pl.when(g + DEPTH < seqs // SUB)
        def _():
            for copy in fetch_suffix(g + DEPTH):
                copy.start()

    size = min(PREFIX, rows)

    def prefix(n, chunk):
        kv, part_no = lax.rem(n, kv_heads), n // kv_heads
        local = pl.ds(pl.multiple_of(part_no * size * group, size * group), size * group)
        q_low = q_ref[kv, pl.ds(pl.multiple_of((chunk * rows + part_no * size) * group, size * group), size * group)].astype(BF16)
        s = lax.dot_general(q_low, kv_all[:, 0, kv].reshape(n_ctx * positions, dim), LAST, preferred_element_type=F32)
        top_pre = jnp.max(s, axis=-1, keepdims=True)
        e = jnp.exp2((s - top_pre) * factor)
        total_pre = jnp.sum(e, axis=-1, keepdims=True)
        o_pre = jnp.dot(e.astype(BF16), kv_all[:, 1, kv].reshape(n_ctx * positions, dim), preferred_element_type=F32)
        top_suf = m_suf[kv, local]
        top = jnp.maximum(top_pre, top_suf)
        w_pre = jnp.exp2((top_pre - top) * factor)
        w_suf = jnp.exp2((top_suf - top) * factor)
        total = w_pre * total_pre + w_suf * l_suf[kv, local]
        flat[...] = (w_pre * o_pre + w_suf * o_suf[kv, local]) / total
        where = pl.ds(pl.multiple_of(chunk * rows + part_no * size, size), size)
        for h in range(group):
            cols = pl.ds(pl.multiple_of((kv * group + h) * dim, dim), dim)
            att_ref[where, cols] = flat[pl.ds(h, size, stride=group), :].astype(BF16)

    def attend(chunk):
        def body(i, carry):
            suffix(chunk * (rows // SUB) + i, chunk)
            return carry

        lax.fori_loop(0, rows // SUB, body, 0)
        if chunk == 0:
            for index, slot in enumerate((here, x_left, x_right, x_far)):
                other = kv_all.at[slot + partner - here]
                pltpu.make_async_remote_copy(src_ref=other, dst_ref=other, send_sem=pair_send.at[index], recv_sem=pair_recv.at[index], device_id={'ctx': partner}, device_id_type=MESH).wait_recv()

        def body_pre(n, carry):
            prefix(n, chunk)
            return carry

        lax.fori_loop(0, kv_heads * (rows // size), body_pre, 0)

    def copy(kind, way, p, src, dst):
        return pltpu.make_async_remote_copy(src_ref=src, dst_ref=dst, send_sem=send_sem.at[kind, way, p], recv_sem=recv_sem.at[kind, way, p], device_id={'tp': (right, left)[way]}, device_id_type=MESH)

    def span(p):
        return pl.ds(p * step, step)

    started = []

    def launch(*args):
        one = copy(*args)
        one.start()
        started.append(one)

    def mine(chunk):
        return range(chunk * per, (chunk + 1) * per)

    def project_out(chunk, k0, k1):
        which = pl.ds(chunk * rows, rows)

        def body(n, carry):
            k, t = n // tiles, lax.rem(n, tiles)
            slot = lax.rem(k + blocks - bufs, bufs)
            if chunk == 0:
                @pl.when(t == 0)
                def _():
                    weights_here(slot)
            part[k, which, pl.ds(pl.multiple_of(t * width, width), width)] = jnp.dot(att_ref[which, :], pool[slot, pl.ds(pl.multiple_of(t * inner, inner), inner), :], preferred_element_type=F32)
            return carry

        lax.fori_loop(k0 * tiles, k1 * tiles, body, 0)

    def send_parts(chunk):
        project_out(chunk, 0, 1)
        for p in mine(chunk):
            launch(0, 1, p, part.at[0, span(p)], first_in.at[1, span(p)])
        project_out(chunk, 1, 2)
        for p in mine(chunk):
            launch(0, 0, p, part.at[1, span(p)], first_in.at[0, span(p)])
        project_out(chunk, 2, 4)
        for p in mine(chunk):
            launch(1, 0, p, part.at[2, span(p)], direct_in.at[0, span(p)])
            launch(1, 1, p, part.at[3, span(p)], direct_in.at[1, span(p)])
        project_out(chunk, 4, 8)

    def forward_sums(chunk):
        for p in mine(chunk):
            for way, k in ((0, 4), (1, 5)):
                copy(0, way, p, first_in.at[way, span(p)], first_in.at[way, span(p)]).wait_recv()
                part[k, span(p)] += first_in[way, span(p)]
                launch(2, way, p, part.at[k, span(p)], sum_in.at[way, span(p)])

    def finish(chunk):
        for p in mine(chunk):
            for way in (0, 1):
                copy(1, way, p, direct_in.at[way, span(p)], direct_in.at[way, span(p)]).wait_recv()
                copy(2, way, p, sum_in.at[way, span(p)], sum_in.at[way, span(p)]).wait_recv()
            for which in (0, 1):
                total = part[6 + which, span(p)] + sum_in[1 - which, span(p)] + direct_in[which, span(p)]
                total = total + x_ref[span(p), columns(me, which, half)].astype(F32)
                y_ref[span(p), columns(me, which, half)] = total.astype(BF16)
            for way in (0, 1):
                block = y_ref.at[span(p), columns(me, 0, 2 * half)]
                launch(3, way, p, block, block)

    def forward_results(chunk):
        for p in mine(chunk):
            for way, source in ((0, left), (1, right)):
                block = y_ref.at[span(p), columns(source, 0, 2 * half)]
                copy(3, way, p, block, block).wait_recv()
                block = y_ref.at[span(p), columns(source, way, half)]
                launch(4, way, p, block, block)

    for chunk in range(CHUNKS):
        attend(chunk)
        if chunk:
            finish(chunk - 1)
        send_parts(chunk)
        if chunk:
            forward_results(chunk - 1)
        forward_sums(chunk)
    finish(CHUNKS - 1)
    forward_results(CHUNKS - 1)
    for p in range(PIECES):
        for way in (0, 1):
            block = y_ref.at[span(p), columns(far, way, half)]
            copy(4, way, p, block, block).wait_recv()
    for one in started:
        one.wait_send()
    ring(own, own, 0, x_right).wait_send()
    ring(own, own, 1, x_left).wait_send()
    ring(kv_all.at[x_left, 0], kv_all.at[x_left, 0], 2, x_right).wait_send()
    ring(kv_all.at[x_right, 1], kv_all.at[x_right, 1], 3, x_left).wait_send()
    for index, slot in enumerate((here, x_left, x_right, x_far)):
        pair(slot, index).wait_send()


def solution(mesh):
    n_ctx, n_tp = mesh.shape['ctx'], mesh.shape['tp']
    row_axes = ('dp', 'ctx')
    vmem = pl.BlockSpec(memory_space=pltpu.VMEM)
    hbm = pl.BlockSpec(memory_space=pl.ANY)
    dma = pltpu.SemaphoreType.DMA

    def device_step(hidden, w_q, w_k, w_v, w_o, k_prefix, v_prefix, k_suffix, v_suffix, seq_lens):
        seqs, model = hidden.shape
        positions, kv_heads, dim = k_prefix.shape
        slots = k_suffix.shape[1] * kv_heads
        inner = w_q.shape[1]
        group = inner // (kv_heads * dim)
        width = w_k.shape[1]
        half = model // (2 * n_tp)
        rows = seqs // CHUNKS
        size = min(PREFIX, rows)
        return pl.pallas_call(
            functools.partial(layer_kernel, dim ** -0.5, n_ctx, n_tp),
            name='layer',
            out_shape=jax.ShapeDtypeStruct((seqs, model), BF16),
            in_specs=[pl.BlockSpec(memory_space=pltpu.SMEM), vmem, vmem] + [hbm] * 7,
            out_specs=vmem,
            scratch_shapes=[
                pltpu.VMEM((seqs, model), BF16),
                pltpu.VMEM((8, model, width), BF16),
                pltpu.VMEM((n_ctx, 2, kv_heads, positions, dim), BF16),
                pltpu.VMEM((kv_heads, seqs * group, dim), F32),
                pltpu.VMEM((2, kv_heads, seqs, dim), F32),
                pltpu.VMEM((DEPTH, SUB, slots, dim), BF16),
                pltpu.VMEM((DEPTH, SUB, slots, dim), BF16),
                pltpu.VMEM((kv_heads, rows * group, dim), F32),
                pltpu.VMEM((kv_heads, rows * group, 1), F32),
                pltpu.VMEM((kv_heads, rows * group, 1), F32),
                pltpu.VMEM((size * group, dim), F32),
                pltpu.VMEM((seqs, inner), BF16),
                pltpu.VMEM((8, seqs, half), F32),
                pltpu.VMEM((2, seqs, half), F32),
                pltpu.VMEM((2, seqs, half), F32),
                pltpu.VMEM((2, seqs, half), F32),
                dma, dma((8,)), dma((DEPTH,)), dma((DEPTH,)), dma((4,)), dma((4,)), dma((4,)), dma((4,)), dma((5, 2, PIECES)), dma((5, 2, PIECES)),
            ],
            compiler_params=pltpu.CompilerParams(collective_id=0, has_side_effects=True, vmem_limit_bytes=67000000),
        )(seq_lens, k_prefix.reshape(positions * kv_heads, dim), v_prefix.reshape(positions * kv_heads, dim), hidden, w_q, w_k, w_v, w_o, k_suffix.reshape(seqs, slots, dim), v_suffix.reshape(seqs, slots, dim))

    spec_in = (P(row_axes, None), P(None, 'tp'), P(None, 'tp'), P(None, 'tp'), P('tp', None), P(row_axes, 'tp', None), P(row_axes, 'tp', None), P(row_axes, None, 'tp', None), P(row_axes, None, 'tp', None), P(row_axes))
    return jax.shard_map(device_step, mesh=mesh, in_specs=spec_in, out_specs=P(row_axes, None), check_vma=False)
```

time: 473 us -> 102 us (0.22); the launches traced: 465 us -> 100 us
  waiting for transfers between devices: 283 us -> 0 us
  Pallas kernels: 0 us -> 97.1 us
  matrix products: 78.1 us -> 0 us
  local copies, waits for them, and re-layouts: 50.4 us -> 3.1 us
  other arithmetic: 33.6 us -> 0 us
  between operations: 14 us -> 0.01 us
  starting transfers between devices: 6.05 us -> 0 us
    all_to_all x1 -> x0, waiting for transfers between devices: 162 us -> none  [device_step(): returned = lax.all_to_all(partial_state, 'ctx', 0, 0, tiled=True)]
    pallas_call x0 -> x1, Pallas kernels: none -> 97.1 us  [device_step(): pl.pallas_call(functools.partial(layer_kernel, dim ** (-0.5), n_ctx, n_tp...]
    psum x1 -> x0, waiting for transfers between devices: 87.2 us -> none  [device_step(): out_hidden = hidden.astype(jnp.float32) + lax.psum(proj_part, 'tp')]
    dot_general x9 -> x0, matrix products: 78.1 us -> none  [the longest x1 17.1 us: device_step(): proj_part = jnp.dot(attn_out, w_o, preferred_element_type=jnp.float32)]
    all_gather x1 -> x0, waiting for transfers between devices: 33.7 us -> none  [device_step(): q_every = lax.all_gather(q_local, 'ctx', axis=0, tiled=True)]
    concatenate x1 -> x0, local copies, waits for them, and re-layouts: 17.7 us -> none  [device_step(): jnp.concatenate([o_pre / l_pre[..., None], (m_pre + jnp.log(l_pre))[...,...]
    reduce_sum x4 -> x0, other arithmetic: 17.6 us -> none  [the longest x1 8.65 us: device_step(): l_pre = jnp.sum(e_pre, axis=-1)]
    unnamed x14 -> x1, local copies, waits for them, and re-layouts: 19.4 us -> 3.1 us
  transfers between devices with their start and end apart: 3 -> 0, of which waited for: 3 -> 0; matrix products, arithmetic and copies ran while one was open for 5% -> 0% of each run, Pallas kernels for 0% -> 0%
where the time goes in v2:
time: 102 us; the launch traced here: 100 us
  Pallas kernels  97.1 us (95%)
  local copies, waits for them, and re-layouts  3.1 us (3%)
    pallas_call x1, Pallas kernels, device_step(): pl.pallas_call(functools.partial(layer_kernel, dim ** (-0.5), n_ctx, n_tp...  97.1 us
    unnamed x1, local copies, waits for them, and re-layouts  3.1 us

profile of v2, /device:TPU:97, one launch (start us, length us, event | category | flops | bytes accessed | tf_op | source)
XLA Modules:
  0.0 100.2 jit_solution(17314162427241828865)
XLA Ops:
  0.0 97.1 %layer.1 = bf16[128,8192]{1,0:T(8,128)(2,1)} custom-call(s32[128]{0:T(128)} %len_ref.1, bf16[512,128]{1,0:T(8,128)(2,1)} %bitcast.6, bf16[512,128]{1,0:T(8,128)(2,1)} %bitcast.7, bf16[128,8192]{1,0:T(8,128)(2,1)} %x_hbm.1, bf16[8192,2048]{1,0:T(8,128)(2,1)} %wq_hbm.1, bf16[8192,256]{1,0:T(8,128)(2,1)} %wk_hbm.1, bf16[8192,256]{1,0:T(8,128)(2,1)} %wv_hbm.1, ...), custom_call_target="tpu_custom_call" | custom-call | tf_op jit(solution)/shard_map/layer/pallas_call | solution.py:351
  97.1 3.1 %copy.12 = bf16[128,8192]{1,0:T(8,128)(2,1)} copy(bf16[128,8192]{1,0:T(8,128)(2,1)} %layer.1) | data formatting | bytes 4194304

commit v3 on v2

--- a/solution.py
+++ b/solution.py
@@ -14,15 +14,16 @@
 
 ORDER = ((2, 0), (2, 1), (1, 0), (3, 1), (1, 1), (3, 0), (0, 0), (0, 1))
 SUB = 8
-DEPTH = 3
+EARLY = 2
+DEPTH = 4
 PREFIX = 32
-CHUNKS = 2
-PIECES = 4
-
-
-def layer_kernel(scale, n_ctx, n_tp, len_ref, kp_ref, vp_ref, x_hbm, wq_hbm, wk_hbm, wv_hbm, wo_hbm, ks_hbm, vs_hbm, y_ref,
-                 x_ref, pool, kv_all, q_ref, new_ref, kbuf, vbuf, o_suf, m_suf, l_suf, flat, att_ref, part, first_in, direct_in, sum_in,
-                 x_sem, wsem, ksem, vsem, ring_send, ring_recv, pair_send, pair_recv, send_sem, recv_sem):
+CHUNKS = 4
+PIECES = 8
+
+
+def layer_kernel(scale, n_ctx, n_tp, len_ref, kp_ref, vp_ref, x_hbm, wq_hbm, wk_hbm, wv_hbm, wo_hbm, ks_hbm, vs_hbm, y_hbm,
+                 y_ref, x_ref, pool, kv_all, q_ref, new_ref, kbuf, vbuf, o_suf, m_suf, l_suf, flat, att_ref, part, first_in, direct_in, sum_in,
+                 x_sem, y_sem, wsem, ksem, vsem, ring_send, ring_recv, pair_send, pair_recv, send_sem, recv_sem):
     kv_heads, positions, dim = kv_all.shape[2:]
     seqs = x_ref.shape[0]
     model, width = wk_hbm.shape
@@ -135,7 +136,7 @@
                 for copy in fetch_suffix(jnp.int32(g)):
                     copy.start()
 
-        @pl.when(j >= blocks - bufs)
+        @pl.when((j >= blocks - bufs) & (j < blocks - bufs + EARLY))
         def _():
             fetch_o(j - (blocks - bufs), slot)
 
@@ -196,6 +197,14 @@
             for copy in fetch_suffix(g + DEPTH):
                 copy.start()
 
+        share = -(-(8 - EARLY) // (rows // SUB))
+        for i in range(share):
+            k = EARLY + g * share + i
+
+            @pl.when((g < rows // SUB) & (k < 8))
+            def _():
+                fetch_o(k, lax.rem(k + blocks - bufs, bufs))
+
     size = min(PREFIX, rows)
 
     def prefix(n, chunk):
@@ -224,7 +233,9 @@
             return carry
 
         lax.fori_loop(0, rows // SUB, body, 0)
-        if chunk == 0:
+
+        @pl.when(chunk == 0)
+        def _():
             for index, slot in enumerate((here, x_left, x_right, x_far)):
                 other = kv_all.at[slot + partner - here]
                 pltpu.make_async_remote_copy(src_ref=other, dst_ref=other, send_sem=pair_send.at[index], recv_sem=pair_recv.at[index], device_id={'ctx': partner}, device_id_type=MESH).wait_recv()
@@ -238,97 +249,155 @@
     def copy(kind, way, p, src, dst):
         return pltpu.make_async_remote_copy(src_ref=src, dst_ref=dst, send_sem=send_sem.at[kind, way, p], recv_sem=recv_sem.at[kind, way, p], device_id={'tp': (right, left)[way]}, device_id_type=MESH)
 
+    def here_only(kind, way, p, ref):
+        return copy(kind, way, p, ref, ref)
+
     def span(p):
-        return pl.ds(p * step, step)
-
-    started = []
-
-    def launch(*args):
-        one = copy(*args)
-        one.start()
-        started.append(one)
-
-    def mine(chunk):
-        return range(chunk * per, (chunk + 1) * per)
+        return pl.ds(pl.multiple_of(p * step, step), step)
+
+    def pieces_of(chunk, action):
+        def body(p, carry):
+            action(p)
+            return carry
+
+        lax.fori_loop(chunk * per, (chunk + 1) * per, body, 0)
+
+    def first(way, p):
+        return copy(0, way, p, part.at[1 - way, span(p)], first_in.at[way, span(p)])
+
+    def direct(way, p):
+        return copy(1, way, p, part.at[2 + way, span(p)], direct_in.at[way, span(p)])
+
+    def summed(way, p):
+        return copy(2, way, p, part.at[4 + way, span(p)], sum_in.at[way, span(p)])
+
+    def result(way, p, owner):
+        return here_only(3, way, p, y_ref.at[span(p), columns(owner, 0, 2 * half)])
+
+    def passed_on(way, p, owner):
+        return here_only(4, way, p, y_ref.at[span(p), columns(owner, way, half)])
 
     def project_out(chunk, k0, k1):
-        which = pl.ds(chunk * rows, rows)
+        which = pl.ds(pl.multiple_of(chunk * rows, rows), rows)
 
         def body(n, carry):
             k, t = n // tiles, lax.rem(n, tiles)
             slot = lax.rem(k + blocks - bufs, bufs)
-            if chunk == 0:
-                @pl.when(t == 0)
-                def _():
-                    weights_here(slot)
+
+            @pl.when((chunk == 0) & (t == 0))
+            def _():
+                weights_here(slot)
+
             part[k, which, pl.ds(pl.multiple_of(t * width, width), width)] = jnp.dot(att_ref[which, :], pool[slot, pl.ds(pl.multiple_of(t * inner, inner), inner), :], preferred_element_type=F32)
             return carry
 
         lax.fori_loop(k0 * tiles, k1 * tiles, body, 0)
 
     def send_parts(chunk):
-        project_out(chunk, 0, 1)
-        for p in mine(chunk):
-            launch(0, 1, p, part.at[0, span(p)], first_in.at[1, span(p)])
-        project_out(chunk, 1, 2)
-        for p in mine(chunk):
-            launch(0, 0, p, part.at[1, span(p)], first_in.at[0, span(p)])
-        project_out(chunk, 2, 4)
-        for p in mine(chunk):
-            launch(1, 0, p, part.at[2, span(p)], direct_in.at[0, span(p)])
-            launch(1, 1, p, part.at[3, span(p)], direct_in.at[1, span(p)])
-        project_out(chunk, 4, 8)
+        def go(k, carry):
+            project_out(chunk, k, k + 1)
+
+            @pl.when(k == 0)
+            def _():
+                pieces_of(chunk, lambda p: first(1, p).start())
+
+            @pl.when(k == 1)
+            def _():
+                pieces_of(chunk, lambda p: first(0, p).start())
+
+            @pl.when(k == 3)
+            def _():
+                def both(p):
+                    direct(0, p).start()
+                    direct(1, p).start()
+
+                pieces_of(chunk, both)
+
+            return carry
+
+        lax.fori_loop(0, 8, go, 0)
 
     def forward_sums(chunk):
-        for p in mine(chunk):
-            for way, k in ((0, 4), (1, 5)):
-                copy(0, way, p, first_in.at[way, span(p)], first_in.at[way, span(p)]).wait_recv()
-                part[k, span(p)] += first_in[way, span(p)]
-                launch(2, way, p, part.at[k, span(p)], sum_in.at[way, span(p)])
+        def action(p):
+            for way in (0, 1):
+                first(way, p).wait_recv()
+                part[4 + way, span(p)] += first_in[way, span(p)]
+                summed(way, p).start()
+
+        pieces_of(chunk, action)
 
     def finish(chunk):
-        for p in mine(chunk):
+        def action(p):
             for way in (0, 1):
-                copy(1, way, p, direct_in.at[way, span(p)], direct_in.at[way, span(p)]).wait_recv()
-                copy(2, way, p, sum_in.at[way, span(p)], sum_in.at[way, span(p)]).wait_recv()
+                direct(way, p).wait_recv()
+                summed(way, p).wait_recv()
             for which in (0, 1):
                 total = part[6 + which, span(p)] + sum_in[1 - which, span(p)] + direct_in[which, span(p)]
                 total = total + x_ref[span(p), columns(me, which, half)].astype(F32)
                 y_ref[span(p), columns(me, which, half)] = total.astype(BF16)
             for way in (0, 1):
-                block = y_ref.at[span(p), columns(me, 0, 2 * half)]
-                launch(3, way, p, block, block)
+                result(way, p, me).start()
+
+        pieces_of(chunk, action)
 
     def forward_results(chunk):
-        for p in mine(chunk):
+        def action(p):
             for way, source in ((0, left), (1, right)):
-                block = y_ref.at[span(p), columns(source, 0, 2 * half)]
-                copy(3, way, p, block, block).wait_recv()
-                block = y_ref.at[span(p), columns(source, way, half)]
-                launch(4, way, p, block, block)
-
-    for chunk in range(CHUNKS):
-        attend(chunk)
-        if chunk:
-            finish(chunk - 1)
-        send_parts(chunk)
-        if chunk:
-            forward_results(chunk - 1)
-        forward_sums(chunk)
-    finish(CHUNKS - 1)
-    forward_results(CHUNKS - 1)
-    for p in range(PIECES):
+                result(way, p, source).wait_recv()
+                passed_on(way, p, source).start()
+
+        pieces_of(chunk, action)
+
+    def pipeline(stage, carry):
+        @pl.when(stage < CHUNKS)
+        def _():
+            attend(stage)
+
+        @pl.when((stage >= 1) & (stage <= CHUNKS))
+        def _():
+            forward_sums(stage - 1)
+
+        @pl.when((stage >= 2) & (stage <= CHUNKS + 1))
+        def _():
+            finish(stage - 2)
+
+        @pl.when(stage < CHUNKS)
+        def _():
+            send_parts(stage)
+
+        @pl.when(stage >= 3)
+        def _():
+            forward_results(stage - 3)
+
+        return carry
+
+    lax.fori_loop(0, CHUNKS + 3, pipeline, 0)
+
+    def last(p, carry):
         for way in (0, 1):
-            block = y_ref.at[span(p), columns(far, way, half)]
-            copy(4, way, p, block, block).wait_recv()
-    for one in started:
-        one.wait_send()
+            passed_on(way, p, far).wait_recv()
+        pltpu.make_async_copy(y_ref.at[span(p)], y_hbm.at[span(p)], y_sem).start()
+        return carry
+
+    lax.fori_loop(0, PIECES, last, 0)
+
+    def sent(p, carry):
+        for way, source in ((0, left), (1, right)):
+            first(way, p).wait_send()
+            direct(way, p).wait_send()
+            summed(way, p).wait_send()
+            result(way, p, me).wait_send()
+            passed_on(way, p, source).wait_send()
+        return carry
+
+    lax.fori_loop(0, PIECES, sent, 0)
     ring(own, own, 0, x_right).wait_send()
     ring(own, own, 1, x_left).wait_send()
     ring(kv_all.at[x_left, 0], kv_all.at[x_left, 0], 2, x_right).wait_send()
     ring(kv_all.at[x_right, 1], kv_all.at[x_right, 1], 3, x_left).wait_send()
     for index, slot in enumerate((here, x_left, x_right, x_far)):
         pair(slot, index).wait_send()
+    pltpu.make_async_copy(y_ref, y_hbm, y_sem).wait()
 
 
 def solution(mesh):
@@ -353,8 +422,9 @@
             name='layer',
             out_shape=jax.ShapeDtypeStruct((seqs, model), BF16),
             in_specs=[pl.BlockSpec(memory_space=pltpu.SMEM), vmem, vmem] + [hbm] * 7,
-            out_specs=vmem,
+            out_specs=hbm,
             scratch_shapes=[
+                pltpu.VMEM((seqs, model), BF16),
                 pltpu.VMEM((seqs, model), BF16),
                 pltpu.VMEM((8, model, width), BF16),
                 pltpu.VMEM((n_ctx, 2, kv_heads, positions, dim), BF16),
@@ -371,7 +441,7 @@
                 pltpu.VMEM((2, seqs, half), F32),
                 pltpu.VMEM((2, seqs, half), F32),
                 pltpu.VMEM((2, seqs, half), F32),
-                dma, dma((8,)), dma((DEPTH,)), dma((DEPTH,)), dma((4,)), dma((4,)), dma((4,)), dma((4,)), dma((5, 2, PIECES)), dma((5, 2, PIECES)),
+                dma, dma, dma((8,)), dma((DEPTH,)), dma((DEPTH,)), dma((4,)), dma((4,)), dma((4,)), dma((4,)), dma((5, 2, PIECES)), dma((5, 2, PIECES)),
             ],
             compiler_params=pltpu.CompilerParams(collective_id=0, has_side_effects=True, vmem_limit_bytes=67000000),
         )(seq_lens, k_prefix.reshape(positions * kv_heads, dim), v_prefix.reshape(positions * kv_heads, dim), hidden, w_q, w_k, w_v, w_o, k_suffix.reshape(seqs, slots, dim), v_suffix.reshape(seqs, slots, dim))

time: 102 us -> 107 us (1.049)
  Pallas kernels: 97.1 us -> 103 us
    pallas_call x1, Pallas kernels: 97.1 us -> 103 us  [device_step(): pl.pallas_call(functools.partial(layer_kernel, dim ** (-0.5), n_ctx, n_tp...]
where the time goes in v3:
time: 107 us; the launch traced here: 106 us
  Pallas kernels  103 us (96%)
  local copies, waits for them, and re-layouts  3.1 us (3%)
    pallas_call x1, Pallas kernels, device_step(): pl.pallas_call(functools.partial(layer_kernel, dim ** (-0.5), n_ctx, n_tp...  103 us
    unnamed x1, local copies, waits for them, and re-layouts  3.1 us

profile of v3, /device:TPU:97, one launch (start us, length us, event | category | flops | bytes accessed | tf_op | source)
XLA Modules:
  0.0 106.0 jit_solution(13247179322992850294)
XLA Ops:
  0.0 102.9 %layer.1 = bf16[128,8192]{1,0:T(8,128)(2,1)} custom-call(s32[128]{0:T(128)} %len_ref.1, bf16[512,128]{1,0:T(8,128)(2,1)} %bitcast.6, bf16[512,128]{1,0:T(8,128)(2,1)} %bitcast.7, bf16[128,8192]{1,0:T(8,128)(2,1)} %x_hbm.1, bf16[8192,2048]{1,0:T(8,128)(2,1)} %wq_hbm.1, bf16[8192,256]{1,0:T(8,128)(2,1)} %wk_hbm.1, bf16[8192,256]{1,0:T(8,128)(2,1)} %wv_hbm.1, ...), custom_call_target="tpu_custom_call" | custom-call | tf_op jit(solution)/shard_map/layer/pallas_call | solution.py:420
  102.9 3.1 %copy.12 = bf16[128,8192]{1,0:T(8,128)(2,1)} copy(bf16[128,8192]{1,0:T(8,128)(2,1)} %layer.1) | data formatting | bytes 4194304

commit v4 on v3

--- a/solution.py
+++ b/solution.py
@@ -17,7 +17,7 @@
 EARLY = 2
 DEPTH = 4
 PREFIX = 32
-CHUNKS = 4
+CHUNKS = 2
 PIECES = 8
 
 
@@ -197,11 +197,12 @@
             for copy in fetch_suffix(g + DEPTH):
                 copy.start()
 
-        share = -(-(8 - EARLY) // (rows // SUB))
+        begin = max(0, rows // SUB - 4)
+        share = -(-(8 - EARLY) // (rows // SUB - begin))
         for i in range(share):
-            k = EARLY + g * share + i
-
-            @pl.when((g < rows // SUB) & (k < 8))
+            k = EARLY + (g - begin) * share + i
+
+            @pl.when((g >= begin) & (g < rows // SUB) & (k < 8))
             def _():
                 fetch_o(k, lax.rem(k + blocks - bufs, bufs))
 
@@ -353,25 +354,25 @@
         def _():
             attend(stage)
 
-        @pl.when((stage >= 1) & (stage <= CHUNKS))
-        def _():
-            forward_sums(stage - 1)
-
-        @pl.when((stage >= 2) & (stage <= CHUNKS + 1))
-        def _():
-            finish(stage - 2)
+        @pl.when(stage >= 1)
+        def _():
+            finish(stage - 1)
 
         @pl.when(stage < CHUNKS)
         def _():
             send_parts(stage)
 
-        @pl.when(stage >= 3)
-        def _():
-            forward_results(stage - 3)
+        @pl.when(stage >= 1)
+        def _():
+            forward_results(stage - 1)
+
+        @pl.when(stage < CHUNKS)
+        def _():
+            forward_sums(stage)
 
         return carry
 
-    lax.fori_loop(0, CHUNKS + 3, pipeline, 0)
+    lax.fori_loop(0, CHUNKS + 1, pipeline, 0)
 
     def last(p, carry):
         for way in (0, 1):

time: 107 us -> 97.5 us (0.911)
  Pallas kernels: 103 us -> 93.6 us
    pallas_call x1, Pallas kernels: 103 us -> 93.6 us  [device_step(): pl.pallas_call(functools.partial(layer_kernel, dim ** (-0.5), n_ctx, n_tp...]
where the time goes in v4:
time: 97.5 us; the launch traced here: 96.7 us
  Pallas kernels  93.6 us (96%)
  local copies, waits for them, and re-layouts  3.1 us (3%)
    pallas_call x1, Pallas kernels, device_step(): pl.pallas_call(functools.partial(layer_kernel, dim ** (-0.5), n_ctx, n_tp...  93.6 us
    unnamed x1, local copies, waits for them, and re-layouts  3.1 us

profile of v4, /device:TPU:97, one launch (start us, length us, event | category | flops | bytes accessed | tf_op | source)
XLA Modules:
  0.0 96.7 jit_solution(14135067333105852964)
XLA Ops:
  0.0 93.6 %layer.1 = bf16[128,8192]{1,0:T(8,128)(2,1)} custom-call(s32[128]{0:T(128)} %len_ref.1, bf16[512,128]{1,0:T(8,128)(2,1)} %bitcast.6, bf16[512,128]{1,0:T(8,128)(2,1)} %bitcast.7, bf16[128,8192]{1,0:T(8,128)(2,1)} %x_hbm.1, bf16[8192,2048]{1,0:T(8,128)(2,1)} %wq_hbm.1, bf16[8192,256]{1,0:T(8,128)(2,1)} %wk_hbm.1, bf16[8192,256]{1,0:T(8,128)(2,1)} %wv_hbm.1, ...), custom_call_target="tpu_custom_call" | custom-call | tf_op jit(solution)/shard_map/layer/pallas_call | solution.py:421
  93.6 3.1 %copy.12 = bf16[128,8192]{1,0:T(8,128)(2,1)} copy(bf16[128,8192]{1,0:T(8,128)(2,1)} %layer.1) | data formatting | bytes 4194304
